TPU v7x, 32 devices: a whole 2x2x4 slice. The times are simulated.
32 devices in a mesh: ctx: 4 (over x, core), section: 8 (over z, y).
Axes of the slice: x: 2, y: 2, z: 4, core: 2. Of those that a mesh axis runs over, the one named last changes fastest.
Arguments:
- query_in: bfloat16 [8, 2, 512, 1024], P('section', None, 'ctx'), may hold values from -200 to 200
- key_in: bfloat16 [8, 2, 512, 128], P('section', None, 'ctx'), may hold values from -5 to 5
- value_in: bfloat16 [8, 2, 512, 128], P('section', None, 'ctx'), may hold values from -24 to 24
- forward_out: bfloat16 [8, 2, 512, 1024], P('section', None, 'ctx'), may hold values from -6 to 6
- log_sum: float32 [8, 2, 8, 512], P('section', None, None, 'ctx'), as said below
- grad_out: bfloat16 [8, 2, 512, 1024], P('section', None, 'ctx'), may hold values from -6 to 6
- block_order: int32 [8], replicated, may hold values from 0 to 7, each once
Outputs:
- grad_query: bfloat16 [8, 2, 512, 1024], P('section', None, 'ctx')
- grad_key: bfloat16 [8, 2, 512, 128], P('section', None, 'ctx')
- grad_value: bfloat16 [8, 2, 512, 128], P('section', None, 'ctx')
Inputs may be any that keep to these rules, and one draw needn't show every extreme that they name: For every layer, micro-batch, head and row, log_sum is at least the logarithm of the sum of exp(score) over all key rows of that row's window, masked or not. block_order is a permutation: slot j, rows j * 64 to j * 64 + 63 of the token dimension, holds sequence positions block_order[j] * 64 onward in order.
All inputs are finite; a program needn't handle non-finite values.
Results may differ from a plain program's by a relative error of at most 0.008.
Values may be sent and summed in bfloat16 or wider, within the bound.
A program may use at most 64 MiB of HBM per device.

v0:
```python
import functools
import math

import jax
import jax.numpy as jnp
from jax import lax
from jax.experimental import pallas as pl
from jax.experimental.pallas import tpu as pltpu
from jax.sharding import PartitionSpec as P

WINDOW = 3
LOG2E = math.log2(math.e)
HIDE = -1e30


def dot(a, b, dims):
    return lax.dot_general(a, b, (dims, ((), ())), preferred_element_type=jnp.float32)


def kernel(
    members, sections, blocks,
    order_ref, q_hbm, k_hbm, v_hbm, fo_hbm, go_hbm, log_hbm,
    dq, kv_out,
    q, fo, go, logs, kv, bias, passed, own, part, back,
    q_sem, fo_sem, go_sem, log_sem, kv_sem,
    kv_send, kv_recv, part_send, part_recv, hop_send, hop_recv,
):
    micro, rows, width = q.shape
    head = kv.shape[-1]
    chunks, _, wide = passed.shape
    group = wide // head
    span = group * rows
    factor = 1.0 / math.sqrt(head)
    me = lax.axis_index("ctx")
    sec = lax.axis_index("section")
    peer = lambda offset: {"ctx": lax.rem(me + offset + members, members)}
    below = {"section": jnp.maximum(sec - 1, 0)}
    above = {"section": jnp.minimum(sec + 1, sections - 1)}
    has_below = sec > 0
    has_above = sec < sections - 1

    kv_loads, loads = [], []
    for m in range(micro):
        for which, source in enumerate((k_hbm, v_hbm)):
            copy = pltpu.make_async_copy(source.at[0, m], kv.at[m, 0, which], kv_sem.at[m, which])
            copy.start()
            kv_loads.append(copy)
    for m in range(micro):
        now = [
            pltpu.make_async_copy(log_hbm.at[0, m], logs.at[m], log_sem.at[m]),
            pltpu.make_async_copy(q_hbm.at[0, m], q.at[m], q_sem.at[m]),
            pltpu.make_async_copy(go_hbm.at[0, m], go.at[m], go_sem.at[m]),
            pltpu.make_async_copy(fo_hbm.at[0, m], fo.at[m], fo_sem.at[m]),
        ]
        for copy in now:
            copy.start()
        loads.append(now)

    barrier = pltpu.get_barrier_semaphore()
    near = sorted({o % members for o in range(1 - WINDOW, WINDOW)} - {0})
    for o in near:
        pl.semaphore_signal(barrier, inc=1, device_id=peer(o), device_id_type=pl.DeviceIdType.MESH)

    @pl.when(has_below)
    def _():
        pl.semaphore_signal(barrier, inc=1, device_id=below, device_id_type=pl.DeviceIdType.MESH)

    @pl.when(has_above)
    def _():
        pl.semaphore_signal(barrier, inc=1, device_id=above, device_id_type=pl.DeviceIdType.MESH)

    half = members * rows // blocks
    per = rows // half
    lane = lax.broadcasted_iota(jnp.int32, (half, rows), 1)
    down = lax.broadcasted_iota(jnp.int32, (half, rows), 0)
    q_place = lax.rem(lane, half)
    for b in range(per):
        base = order_ref[me * per + b] * half
        q_place = q_place + jnp.where(lane // half == b, base, 0)
    for o in range(WINDOW):
        source = lax.rem(me - o + members, members)
        for b in range(per):
            k_place = down + order_ref[source * per + b] * half
            tile = jnp.where(k_place <= q_place, 0.0, HIDE)
            for g in range(group):
                bias[pl.ds(o * rows + b * half, half), pl.ds(g * rows, rows)] = tile

    @pl.when(jnp.logical_not(has_above))
    def _():
        passed[...] = jnp.zeros_like(passed)

    pl.semaphore_wait(barrier, len(near) + has_below.astype(jnp.int32) + has_above.astype(jnp.int32))

    def send_kv(m):
        copies = []
        for o in range(WINDOW - 1, 0, -1):
            copy = pltpu.make_async_remote_copy(
                src_ref=kv.at[m, 0], dst_ref=kv.at[m, o],
                send_sem=kv_send.at[m, o - 1], recv_sem=kv_recv.at[m, o - 1],
                device_id=peer(o), device_id_type=pl.DeviceIdType.MESH,
            )
            copy.start()
            copies.append(copy)
        return copies

    kv_loads[0].wait()
    kv_loads[1].wait()
    kv_copies = [send_kv(0)]

    ones = jnp.ones((8, head), jnp.bfloat16)
    part_copies = []

    def split(block):
        return jnp.concatenate([block[:, g * head:(g + 1) * head] for g in range(group)], axis=0)

    for m in range(micro):
        for copy in loads[m]:
            copy.wait()
        for copy in kv_copies[m]:
            copy.wait_recv()
        if m == 0:
            for copy in kv_loads[2:]:
                copy.wait()
            for later in range(1, micro):
                kv_copies.append(send_kv(later))
        keys = jnp.concatenate([kv[m, o, 0] for o in range(WINDOW)], axis=0)
        values = jnp.concatenate([kv[m, o, 1] for o in range(WINDOW)], axis=0)
        dk_total = dv_total = None
        for c in range(chunks):
            cols = pl.ds(c * wide, wide)
            queries = split(q[m, :, cols])
            upstream = go[m, :, cols]
            if m > 0:
                if m == 1:
                    @pl.when(has_above)
                    def _(c=c):
                        hop(c).wait_recv()
                upstream = (
                    upstream.astype(jnp.float32) + passed[c].astype(jnp.float32)
                ).astype(jnp.bfloat16)
            upstream = split(upstream)
            product = upstream.astype(jnp.float32) * split(fo[m, :, cols]).astype(jnp.float32)
            high = product.astype(jnp.bfloat16)
            low = (product - high.astype(jnp.float32)).astype(jnp.bfloat16)
            row_dot = (dot(ones, high, ((1,), (1,))) + dot(ones, low, ((1,), (1,))))[0:1]
            log_row = jnp.concatenate(
                [logs[m, pl.ds(c * group + g, 1), :] for g in range(group)], axis=1
            ) * LOG2E
            scores = dot(keys, queries, ((1,), (1,)))
            probs = jnp.exp2(scores * (factor * LOG2E) - log_row + bias[...])
            grad_probs = dot(values, upstream, ((1,), (1,)))
            grad_scores = (probs * (grad_probs - row_dot)).astype(jnp.bfloat16)
            grad_query = dot(grad_scores, keys, ((0,), (0,))) * factor
            for g in range(group):
                dq[m, c, :, pl.ds(g * head, head)] = grad_query[g * rows:(g + 1) * rows].astype(jnp.bfloat16)
            if m == 0:
                def hop(c):
                    return pltpu.make_async_remote_copy(
                        src_ref=dq.at[0, c], dst_ref=passed.at[c],
                        send_sem=hop_send.at[c], recv_sem=hop_recv.at[c],
                        device_id=below, device_id_type=pl.DeviceIdType.MESH,
                    )

                @pl.when(has_below)
                def _(c=c):
                    hop(c).start()
            dk = dot(grad_scores, queries, ((1,), (0,)))
            dv = dot(probs.astype(jnp.bfloat16), upstream, ((1,), (0,)))
            dk_total = dk if dk_total is None else dk_total + dk
            dv_total = dv if dv_total is None else dv_total + dv
        dk_total = dk_total * factor
        for o in range(WINDOW - 1, 0, -1):
            for which, total in enumerate((dk_total, dv_total)):
                part[m, o - 1, which] = total[o * rows:(o + 1) * rows].astype(jnp.bfloat16)
            copy = pltpu.make_async_remote_copy(
                src_ref=part.at[m, o - 1], dst_ref=back.at[m, o - 1],
                send_sem=part_send.at[m, o - 1], recv_sem=part_recv.at[m, o - 1],
                device_id=peer(-o), device_id_type=pl.DeviceIdType.MESH,
            )
            copy.start()
            part_copies.append((m, o, copy))
        own[m, 0] = dk_total[:rows]
        own[m, 1] = dv_total[:rows]

    for m in range(micro):
        for at, o, copy in part_copies:
            if at == m:
                copy.wait_recv()
        for which in range(2):
            total = own[m, which]
            for o in range(1, WINDOW):
                total = total + back[m, o - 1, which].astype(jnp.float32)
            kv_out[m, which] = total.astype(jnp.bfloat16)
    for copies in kv_copies:
        for copy in copies:
            copy.wait_send()
    for _, _, copy in part_copies:
        copy.wait_send()

    @pl.when(has_below)
    def _():
        for c in range(chunks):
            hop(c).wait_send()


def writer(dq, kv_out, dq_hbm, dk_hbm, dv_hbm, dq_sem, kv_sem):
    micro, chunks, _, wide = dq.shape
    copies = []
    for m in range(micro):
        for c in range(chunks):
            copies.append(pltpu.make_async_copy(
                dq.at[m, c], dq_hbm.at[0, m, :, pl.ds(c * wide, wide)], dq_sem.at[m, c]
            ))
        for which, target in enumerate((dk_hbm, dv_hbm)):
            copies.append(pltpu.make_async_copy(
                kv_out.at[m, which], target.at[0, m], kv_sem.at[m, which]
            ))
    for copy in copies:
        copy.start()
    for copy in copies:
        copy.wait()


def solution(mesh):
    members = mesh.shape["ctx"]
    sections = mesh.shape["section"]
    in_specs = (
        P("section", None, "ctx", None),
        P("section", None, "ctx", None),
        P("section", None, "ctx", None),
        P("section", None, "ctx", None),
        P("section", None, None, "ctx"),
        P("section", None, "ctx", None),
        P(),
    )
    out_specs = (
        P("section", None, "ctx", None),
        P("section", None, "ctx", None),
        P("section", None, "ctx", None),
    )

    def shards(query_in, key_in, value_in, forward_out, log_sum, grad_out, block_order):
        _, micro, rows, width = query_in.shape
        head = key_in.shape[3]
        heads = width // head
        group = 2 if heads % 2 == 0 else 1
        chunks = heads // group
        wide = group * head
        low, full = jnp.bfloat16, jnp.float32
        dma = pltpu.SemaphoreType.DMA
        others = WINDOW - 1
        dq, kv_out = pl.pallas_call(
            functools.partial(kernel, members, sections, block_order.shape[0]),
            out_shape=(
                pltpu.VMEM((micro, chunks, rows, wide), low),
                pltpu.VMEM((micro, 2, rows, head), low),
            ),
            in_specs=[pl.BlockSpec(memory_space=pltpu.SMEM)]
            + [pl.BlockSpec(memory_space=pl.ANY)] * 6,
            out_specs=[pl.BlockSpec(memory_space=pltpu.VMEM)] * 2,
            scratch_shapes=[
                pltpu.VMEM((micro, rows, width), low),
                pltpu.VMEM((micro, rows, width), low),
                pltpu.VMEM((micro, rows, width), low),
                pltpu.VMEM((micro, heads, rows), full),
                pltpu.VMEM((micro, WINDOW, 2, rows, head), low),
                pltpu.VMEM((WINDOW * rows, group * rows), full),
                pltpu.VMEM((chunks, rows, wide), low),
                pltpu.VMEM((micro, 2, rows, head), full),
                pltpu.VMEM((micro, others, 2, rows, head), low),
                pltpu.VMEM((micro, others, 2, rows, head), low),
                dma((micro,)), dma((micro,)), dma((micro,)), dma((micro,)), dma((micro, 2)),
                dma((micro, others)), dma((micro, others)),
                dma((micro, others)), dma((micro, others)),
                dma((chunks,)), dma((chunks,)),
            ],
            compiler_params=pltpu.CompilerParams(collective_id=0, has_side_effects=True),
        )(block_order, query_in, key_in, value_in, forward_out, grad_out, log_sum)
        return pl.pallas_call(
            writer,
            out_shape=(
                jax.ShapeDtypeStruct(query_in.shape, low),
                jax.ShapeDtypeStruct(key_in.shape, low),
                jax.ShapeDtypeStruct(value_in.shape, low),
            ),
            in_specs=[pl.BlockSpec(memory_space=pltpu.VMEM)] * 2,
            out_specs=[pl.BlockSpec(memory_space=pl.ANY)] * 3,
            scratch_shapes=[dma((micro, chunks)), dma((micro, 2))],
        )(*(pltpu.with_memory_space_constraint(x, pltpu.VMEM) for x in (dq, kv_out)))

    return jax.shard_map(shards, mesh=mesh, in_specs=in_specs, out_specs=out_specs, check_vma=False)
```

profile of v0, /device:TPU:1, one launch (start us, length us, event | category | flops | bytes accessed | tf_op | source)
XLA Modules:
  0.0 20.9 jit_solution(3003218030649234933)
XLA Ops:
  0.6 19.4 %shard_map.94 = (bf16[2,4,128,256]{3,2,1,0:T(8,128)(2,1)S(1)}, bf16[2,2,128,128]{3,2,1,0:T(8,128)(2,1)S(1)}) custom-call(s32[8]{0:T(128)} %order_ref.1, bf16[1,2,128,1024]{3,2,1,0:T(8,128)(2,1)} %q_hbm.1, bf16[1,2,128,128]{3,2,1,0:T(8,128)(2,1)} %k_hbm.1, bf16[1,2,128,128]{3,2,1,0:T(8,128)(2,1)} %v_hbm.1, bf16[1,2,128,1024]{3,2,1,0:T(8,128)(2,1)} %fo_hbm.1, ...), custom_call_target="tpu_custom_call" | custom-call | tf_op jit(solution)/shard_map/pallas_call | solution.py:252
  20.0 0.9 %shard_map.95 = (bf16[1,2,128,1024]{3,2,1,0:T(8,128)(2,1)}, bf16[1,2,128,128]{3,2,1,0:T(8,128)(2,1)}, bf16[1,2,128,128]{3,2,1,0:T(8,128)(2,1)}) custom-call(bf16[2,4,128,256]{3,2,1,0:T(8,128)(2,1)S(1)} %get-tuple-element.5.dq, bf16[2,2,128,128]{3,2,1,0:T(8,128)(2,1)S(1)} %get-tuple-element.6.kv_out), custom_call_target="tpu_custom_call" | custom-call | tf_op jit(solution)/shard_map/pallas_call | solution.py:279
where the time goes:
time: 21.1 us; the launch traced here: 20.9 us
  Pallas kernels  20.3 us (96%)
  between operations  0.64 us (3%)
    pallas_call x1, Pallas kernels, shards(): pl.pallas_call(functools.partial(kernel, members, sections, block_order.s...  19.4 us
    pallas_call x1, Pallas kernels, shards(): pl.pallas_call(writer, out_shape=(jax.ShapeDtypeStruct(query_in.shape, lo...  0.93 us

commit v1 on v0

v1 whole, which is shorter than its diff:
```python
import functools
import math

import jax
import jax.numpy as jnp
from jax import lax
from jax.experimental import pallas as pl
from jax.experimental.pallas import tpu as pltpu
from jax.sharding import PartitionSpec as P

WINDOW = 3
LOG2E = math.log2(math.e)
HIDE = -1e30


def dot(a, b, dims):
    return lax.dot_general(a, b, (dims, ((), ())), preferred_element_type=jnp.float32)


def kernel(
    members, sections, blocks,
    order_hbm, q_hbm, k_hbm, v_hbm, fo_hbm, go_hbm, log_hbm,
    dq, kv_out,
    rows_in, logs, kv, bias, passed, own, part, back, dq_own, ds, pr, pf, order,
    order_sem, rows_sem, log_sem, kv_sem,
    kv_send, kv_recv, part_send, part_recv, hop_send, hop_recv,
):
    _, micro, rows, width = rows_in.shape
    q, go, fo = rows_in.at[0], rows_in.at[1], rows_in.at[2]
    head = kv.shape[-1]
    chunks, _, wide = passed.shape
    group = wide // head
    span = group * rows
    factor = 1.0 / math.sqrt(head)
    me = lax.axis_index("ctx")
    sec = lax.axis_index("section")
    peer = lambda offset: {"ctx": lax.rem(me + offset + members, members)}
    below = {"section": jnp.maximum(sec - 1, 0)}
    above = {"section": jnp.minimum(sec + 1, sections - 1)}
    has_below = sec > 0
    has_above = sec < sections - 1

    barrier = pltpu.get_barrier_semaphore()
    near = sorted({o % members for o in range(1 - WINDOW, WINDOW)} - {0})
    for o in near:
        pl.semaphore_signal(barrier, inc=1, device_id=peer(o), device_id_type=pl.DeviceIdType.MESH)

    @pl.when(has_above)
    def _():
        pl.semaphore_signal(barrier, inc=1, device_id=above, device_id_type=pl.DeviceIdType.MESH)

    def arrived(ref, sem):
        pltpu.make_async_copy(ref, ref, sem).wait()

    for m in range(micro):
        for which, source in enumerate((k_hbm, v_hbm)):
            pltpu.make_async_copy(source.at[0, m], kv.at[m, 0, which], kv_sem.at[m]).start()
    order_load = pltpu.make_async_copy(order_hbm, order, order_sem)
    order_load.start()
    log_load = pltpu.make_async_copy(log_hbm.at[0], logs, log_sem)
    log_load.start()
    for which, source in enumerate((q_hbm, go_hbm, fo_hbm)):
        pltpu.make_async_copy(source.at[0], rows_in.at[which], rows_sem).start()

    half = members * rows // blocks
    per = rows // half
    lane = lax.broadcasted_iota(jnp.int32, (half, rows), 1)
    down = lax.broadcasted_iota(jnp.int32, (half, rows), 0)
    q_place = lax.rem(lane, half)
    order_load.wait()
    for b in range(per):
        base = order[me * per + b] * half
        q_place = q_place + jnp.where(lane // half == b, base, 0)
    for o in range(WINDOW):
        source = lax.rem(me - o + members, members)
        for b in range(per):
            k_place = down + order[source * per + b] * half
            tile = jnp.where(k_place <= q_place, 0.0, HIDE)
            for g in range(group):
                bias[pl.ds(o * rows + b * half, half), pl.ds(g * rows, rows)] = tile

    @pl.when(jnp.logical_not(has_above))
    def _():
        passed[...] = jnp.zeros_like(passed)

    if True:
        pl.semaphore_wait(barrier, len(near) + has_below.astype(jnp.int32))

    others = pl.ds(1, WINDOW - 1)

    def send_kv(m):
        for o in range(WINDOW - 1, 0, -1):
            pltpu.make_async_remote_copy(
                src_ref=kv.at[m, 0], dst_ref=kv.at[m, o],
                send_sem=kv_send, recv_sem=kv_recv.at[m],
                device_id=peer(o), device_id_type=pl.DeviceIdType.MESH,
            ).start()

    arrived(kv.at[0, 0], kv_sem.at[0])
    send_kv(0)

    ones = jnp.ones((8, head), jnp.bfloat16)
    near_rows = pl.ds(rows, (WINDOW - 1) * rows)
    own_rows = pl.ds(0, rows)

    def split(block):
        return jnp.concatenate([block[:, g * head:(g + 1) * head] for g in range(group)], axis=0)

    def stack(block):
        return jnp.concatenate([block[:, h * head:(h + 1) * head] for h in range(width // head)], axis=0)

    def cols(c):
        return pl.ds(c * wide, wide)

    def lanes(c):
        return pl.ds(c * span, span)

    def queries(m, c):
        return split(q[m, :, cols(c)])

    def row_dots(m, c, upstream):
        product = upstream.astype(jnp.float32) * split(fo[m, :, cols(c)]).astype(jnp.float32)
        high = product.astype(jnp.bfloat16)
        low = (product - high.astype(jnp.float32)).astype(jnp.bfloat16)
        return (dot(ones, high, ((1,), (1,))) + dot(ones, low, ((1,), (1,))))[0:1]

    def probs_of(m, c, keys, where):
        log_row = jnp.concatenate(
            [logs[m, pl.ds(c * group + g, 1), :] for g in range(group)], axis=1
        ) * LOG2E
        scores = dot(keys, queries(m, c), ((1,), (1,)))
        return jnp.exp2(scores * (factor * LOG2E) - log_row + bias[where])

    def far(m, which):
        return jnp.concatenate([kv[m, o, which] for o in range(1, WINDOW)], axis=0)

    def grads_of(probs, values, upstream, row_dot):
        return (probs * (dot(values, upstream, ((1,), (1,))) - row_dot)).astype(jnp.bfloat16)

    def put_dq(m, c, grad_query):
        for g in range(group):
            dq[m, c, :, pl.ds(g * head, head)] = grad_query[g * rows:(g + 1) * rows].astype(jnp.bfloat16)

    def hop(c):
        return pltpu.make_async_remote_copy(
            src_ref=dq.at[0, c], dst_ref=passed.at[c],
            send_sem=hop_send, recv_sem=hop_recv.at[c],
            device_id=below, device_id_type=pl.DeviceIdType.MESH,
        )

    def send_parts(m, dk, dv):
        for o in range(WINDOW - 1, 0, -1):
            for which, total in enumerate((dk, dv)):
                part[m, o - 1, which] = total[(o - 1) * rows:o * rows].astype(jnp.bfloat16)
            pltpu.make_async_remote_copy(
                src_ref=part.at[m, o - 1], dst_ref=back.at[m, o - 1],
                send_sem=part_send, recv_sem=part_recv.at[m],
                device_id=peer(-o), device_id_type=pl.DeviceIdType.MESH,
            ).start()

    def finish(m):
        arrived(back.at[m], part_recv.at[m])
        for which in range(2):
            total = own[m, which]
            for o in range(1, WINDOW):
                total = total + back[m, o - 1, which].astype(jnp.float32)
            kv_out[m, which] = total.astype(jnp.bfloat16)

    if True:
        log_load.wait()
        arrived(rows_in, rows_sem)
    keys, values = kv[0, 0, 0], kv[0, 0, 1]
    row_dot = []
    if True:
        for c in range(chunks):
            upstream = split(go[0, :, cols(c)])
            row_dot.append(row_dots(0, c, upstream))
            probs = probs_of(0, c, keys, own_rows)
            grads = grads_of(probs, values, upstream, row_dot[c])
            pr[own_rows, lanes(c)] = probs.astype(jnp.bfloat16)
            ds[own_rows, lanes(c)] = grads
            dq_own[c] = dot(grads, keys, ((0,), (0,)))

    if True:
        arrived(kv.at[0, others], kv_recv.at[0])
    for m in range(1, micro):
        arrived(kv.at[m, 0], kv_sem.at[m])
        send_kv(m)

    keys, values = far(0, 0), far(0, 1)
    for c in range(chunks):
        if True:
            upstream = split(go[0, :, cols(c)])
            probs = probs_of(0, c, keys, near_rows)
            grads = grads_of(probs, values, upstream, row_dot[c])
            pr[near_rows, lanes(c)] = probs.astype(jnp.bfloat16)
            ds[near_rows, lanes(c)] = grads
            put_dq(0, c, (dq_own[c] + dot(grads, keys, ((0,), (0,)))) * factor)

            @pl.when(has_below)
            def _(c=c):
                hop(c).start()

    if True:
        all_queries, all_upstream = stack(q[0]), stack(go[0])
        dk = dot(ds[...], all_queries, ((1,), (0,))) * factor
        dv = dot(pr[...], all_upstream, ((1,), (0,)))
        send_parts(0, dk[rows:], dv[rows:])
        own[0, 0] = dk[:rows]
        own[0, 1] = dv[:rows]

    for m in range(1, micro):
        if True:
            arrived(kv.at[m, others], kv_recv.at[m])
        keys = jnp.concatenate([kv[m, o, 0] for o in range(WINDOW)], axis=0)
        if True:
            for c in range(chunks):
                pf[:, lanes(c)] = probs_of(m, c, keys, pl.ds(0, WINDOW * rows))

        far_values, own_values = far(m, 1), kv[m, 0, 1]
        dk_far = dv_far = dk_own = dv_own = None
        for c in range(chunks):
            if m == 1:
                @pl.when(has_above)
                def _(c=c):
                    if True:
                        hop(c).wait_recv()
            if True:
                chunk = queries(m, c)
                upstream = split((
                    go[m, :, cols(c)].astype(jnp.float32) + passed[c].astype(jnp.float32)
                ).astype(jnp.bfloat16))
                dots = row_dots(m, c, upstream)
                probs = pf[near_rows, lanes(c)]
                grads = grads_of(probs, far_values, upstream, dots)
                dk = dot(grads, chunk, ((1,), (0,)))
                dv = dot(probs.astype(jnp.bfloat16), upstream, ((1,), (0,)))
                dk_far = dk if dk_far is None else dk_far + dk
                dv_far = dv if dv_far is None else dv_far + dv
                if c == chunks - 1:
                    send_parts(m, dk_far * factor, dv_far)
            if True:
                probs = pf[own_rows, lanes(c)]
                own_grads = grads_of(probs, own_values, upstream, dots)
                dk = dot(own_grads, chunk, ((1,), (0,)))
                dv = dot(probs.astype(jnp.bfloat16), upstream, ((1,), (0,)))
                dk_own = dk if dk_own is None else dk_own + dk
                dv_own = dv if dv_own is None else dv_own + dv
                put_dq(m, c, dot(jnp.concatenate([own_grads, grads], axis=0), keys, ((0,), (0,))) * factor)
        own[m, 0] = dk_own * factor
        own[m, 1] = dv_own

    for m in range(micro):
        if True:
            finish(m)
    arrived(kv.at[:, others], kv_send)
    arrived(part, part_send)

    @pl.when(has_below)
    def _():
        arrived(passed, hop_send)


def writer(dq, kv_out, dq_hbm, dk_hbm, dv_hbm, sem):
    micro, chunks, _, wide = dq.shape
    for m in range(micro):
        for c in range(chunks):
            pltpu.make_async_copy(
                dq.at[m, c], dq_hbm.at[0, m, :, pl.ds(c * wide, wide)], sem.at[0]
            ).start()
        for which, target in enumerate((dk_hbm, dv_hbm)):
            pltpu.make_async_copy(kv_out.at[m, which], target.at[0, m], sem.at[1]).start()
    pltpu.make_async_copy(dq, dq, sem.at[0]).wait()
    pltpu.make_async_copy(kv_out, kv_out, sem.at[1]).wait()


def solution(mesh):
    members = mesh.shape["ctx"]
    sections = mesh.shape["section"]
    in_specs = (
        P("section", None, "ctx", None),
        P("section", None, "ctx", None),
        P("section", None, "ctx", None),
        P("section", None, "ctx", None),
        P("section", None, None, "ctx"),
        P("section", None, "ctx", None),
        P(),
    )
    out_specs = (
        P("section", None, "ctx", None),
        P("section", None, "ctx", None),
        P("section", None, "ctx", None),
    )

    def shards(query_in, key_in, value_in, forward_out, log_sum, grad_out, block_order):
        _, micro, rows, width = query_in.shape
        head = key_in.shape[3]
        heads = width // head
        group = 2 if heads % 2 == 0 else 1
        chunks = heads // group
        wide = group * head
        low, full = jnp.bfloat16, jnp.float32
        dma = pltpu.SemaphoreType.DMA
        others = WINDOW - 1
        dq, kv_out = pl.pallas_call(
            functools.partial(kernel, members, sections, block_order.shape[0]),
            out_shape=(
                pltpu.VMEM((micro, chunks, rows, wide), low),
                pltpu.VMEM((micro, 2, rows, head), low),
            ),
            in_specs=[pl.BlockSpec(memory_space=pl.ANY)] * 7,
            out_specs=[pl.BlockSpec(memory_space=pltpu.VMEM)] * 2,
            scratch_shapes=[
                pltpu.VMEM((3, micro, rows, width), low),
                pltpu.VMEM((micro, heads, rows), full),
                pltpu.VMEM((micro, WINDOW, 2, rows, head), low),
                pltpu.VMEM((WINDOW * rows, group * rows), full),
                pltpu.VMEM((chunks, rows, wide), low),
                pltpu.VMEM((micro, 2, rows, head), full),
                pltpu.VMEM((micro, others, 2, rows, head), low),
                pltpu.VMEM((micro, others, 2, rows, head), low),
                pltpu.VMEM((chunks, group * rows, head), full),
                pltpu.VMEM((WINDOW * rows, heads * rows), low),
                pltpu.VMEM((WINDOW * rows, heads * rows), low),
                pltpu.VMEM((WINDOW * rows, heads * rows), full),
                pltpu.SMEM(block_order.shape, jnp.int32),
                dma, dma, dma, dma((micro,)),
                dma, dma((micro,)), dma, dma((micro,)), dma, dma((chunks,)),
            ],
            compiler_params=pltpu.CompilerParams(collective_id=0, has_side_effects=True),
        )(block_order, query_in, key_in, value_in, forward_out, grad_out, log_sum)
        return pl.pallas_call(
            writer,
            out_shape=(
                jax.ShapeDtypeStruct(query_in.shape, low),
                jax.ShapeDtypeStruct(key_in.shape, low),
                jax.ShapeDtypeStruct(value_in.shape, low),
            ),
            in_specs=[pl.BlockSpec(memory_space=pltpu.VMEM)] * 2,
            out_specs=[pl.BlockSpec(memory_space=pl.ANY)] * 3,
            scratch_shapes=[dma((2,))],
        )(*(pltpu.with_memory_space_constraint(x, pltpu.VMEM) for x in (dq, kv_out)))

    return jax.shard_map(shards, mesh=mesh, in_specs=in_specs, out_specs=out_specs, check_vma=False)
```

time: 21.1 us -> 19.9 us (0.943)
  Pallas kernels: 20.3 us -> 19.1 us
    pallas_call x1, Pallas kernels: 19.4 us -> 18.3 us  [shards(): pl.pallas_call(functools.partial(kernel, members, sections, block_order.s...]
where the time goes in v1:
time: 19.9 us; the launch traced here: 19.8 us
  Pallas kernels  19.1 us (96%)
  between operations  0.64 us (3%)
    pallas_call x1, Pallas kernels, shards(): pl.pallas_call(functools.partial(kernel, members, sections, block_order.s...  18.3 us
    pallas_call x1, Pallas kernels, shards(): pl.pallas_call(writer, out_shape=(jax.ShapeDtypeStruct(query_in.shape, lo...  0.84 us

profile of v1, /device:TPU:1, one launch (start us, length us, event | category | flops | bytes accessed | tf_op | source)
XLA Modules:
  0.0 19.8 jit_solution(8521002277890732150)
XLA Ops:
  0.6 18.3 %shard_map.94 = (bf16[2,4,128,256]{3,2,1,0:T(8,128)(2,1)S(1)}, bf16[2,2,128,128]{3,2,1,0:T(8,128)(2,1)S(1)}) custom-call(s32[8]{0:T(128)} %order_hbm.1, bf16[1,2,128,1024]{3,2,1,0:T(8,128)(2,1)} %q_hbm.1, bf16[1,2,128,128]{3,2,1,0:T(8,128)(2,1)} %k_hbm.1, bf16[1,2,128,128]{3,2,1,0:T(8,128)(2,1)} %v_hbm.1, bf16[1,2,128,1024]{3,2,1,0:T(8,128)(2,1)} %fo_hbm.1, ...), custom_call_target="tpu_custom_call" | custom-call | tf_op jit(solution)/shard_map/pallas_call | solution.py:305
  18.9 0.8 %shard_map.95 = (bf16[1,2,128,1024]{3,2,1,0:T(8,128)(2,1)}, bf16[1,2,128,128]{3,2,1,0:T(8,128)(2,1)}, bf16[1,2,128,128]{3,2,1,0:T(8,128)(2,1)}) custom-call(bf16[2,4,128,256]{3,2,1,0:T(8,128)(2,1)S(1)} %get-tuple-element.5.dq, bf16[2,2,128,128]{3,2,1,0:T(8,128)(2,1)S(1)} %get-tuple-element.6.kv_out), custom_call_target="tpu_custom_call" | custom-call | tf_op jit(solution)/shard_map/pallas_call | solution.py:332

commit v2 on v1

--- a/solution.py
+++ b/solution.py
@@ -9,6 +9,8 @@
 from jax.sharding import PartitionSpec as P
 
 WINDOW = 3
+KEEP = 2
+AFTER = {2: 1, 3: 1}
 LOG2E = math.log2(math.e)
 HIDE = -1e30
 
@@ -21,9 +23,9 @@
     members, sections, blocks,
     order_hbm, q_hbm, k_hbm, v_hbm, fo_hbm, go_hbm, log_hbm,
     dq, kv_out,
-    rows_in, logs, kv, bias, passed, own, part, back, dq_own, ds, pr, pf, order,
+    rows_in, logs, kv, bias, passed, own, part, back, dq_own, ds, pr, pf, far_sum, order,
     order_sem, rows_sem, log_sem, kv_sem,
-    kv_send, kv_recv, part_send, part_recv, hop_send, hop_recv,
+    kv_send, k_recv, v_recv, part_send, part_recv, relay_recv, hop_send, hop_recv,
 ):
     _, micro, rows, width = rows_in.shape
     q, go, fo = rows_in.at[0], rows_in.at[1], rows_in.at[2]
@@ -39,6 +41,7 @@
     above = {"section": jnp.minimum(sec + 1, sections - 1)}
     has_below = sec > 0
     has_above = sec < sections - 1
+    first = lax.rem(me, 2) == 0
 
     barrier = pltpu.get_barrier_semaphore()
     near = sorted({o % members for o in range(1 - WINDOW, WINDOW)} - {0})
@@ -61,6 +64,38 @@
     log_load.start()
     for which, source in enumerate((q_hbm, go_hbm, fo_hbm)):
         pltpu.make_async_copy(source.at[0], rows_in.at[which], rows_sem).start()
+
+    if True:
+        pl.semaphore_wait(barrier, len(near) + has_below.astype(jnp.int32))
+
+    others = pl.ds(1, WINDOW - 1)
+    far_recv = (k_recv, v_recv)
+
+    def move_kv(m, source, which, offset, slot):
+        pltpu.make_async_remote_copy(
+            src_ref=kv.at[m, source, which], dst_ref=kv.at[m, slot, which],
+            send_sem=kv_send, recv_sem=far_recv[which].at[m],
+            device_id=peer(offset), device_id_type=pl.DeviceIdType.MESH,
+        ).start()
+
+    def send_kv(m):
+        for which in range(2):
+            move_kv(m, 0, which, 2, 2)
+
+        @pl.when(first)
+        def _():
+            for which in range(2):
+                move_kv(m, 0, which, 1, 1)
+
+    def take_kv(m, which):
+        arrived(kv.at[m, others, which], far_recv[which].at[m])
+
+        @pl.when(jnp.logical_not(first))
+        def _():
+            move_kv(m, 2, which, -1, 1)
+
+    arrived(kv.at[0, 0], kv_sem.at[0])
+    send_kv(0)
 
     half = members * rows // blocks
     per = rows // half
@@ -83,22 +118,6 @@
     def _():
         passed[...] = jnp.zeros_like(passed)
 
-    if True:
-        pl.semaphore_wait(barrier, len(near) + has_below.astype(jnp.int32))
-
-    others = pl.ds(1, WINDOW - 1)
-
-    def send_kv(m):
-        for o in range(WINDOW - 1, 0, -1):
-            pltpu.make_async_remote_copy(
-                src_ref=kv.at[m, 0], dst_ref=kv.at[m, o],
-                send_sem=kv_send, recv_sem=kv_recv.at[m],
-                device_id=peer(o), device_id_type=pl.DeviceIdType.MESH,
-            ).start()
-
-    arrived(kv.at[0, 0], kv_sem.at[0])
-    send_kv(0)
-
     ones = jnp.ones((8, head), jnp.bfloat16)
     near_rows = pl.ds(rows, (WINDOW - 1) * rows)
     own_rows = pl.ds(0, rows)
@@ -148,23 +167,36 @@
             device_id=below, device_id_type=pl.DeviceIdType.MESH,
         )
 
+    def send_part(m, o, offset, recv_sem):
+        pltpu.make_async_remote_copy(
+            src_ref=part.at[m, o - 1], dst_ref=back.at[m, o - 1],
+            send_sem=part_send, recv_sem=recv_sem,
+            device_id=peer(offset), device_id_type=pl.DeviceIdType.MESH,
+        ).start()
+
     def send_parts(m, dk, dv):
         for o in range(WINDOW - 1, 0, -1):
             for which, total in enumerate((dk, dv)):
                 part[m, o - 1, which] = total[(o - 1) * rows:o * rows].astype(jnp.bfloat16)
-            pltpu.make_async_remote_copy(
-                src_ref=part.at[m, o - 1], dst_ref=back.at[m, o - 1],
-                send_sem=part_send, recv_sem=part_recv.at[m],
-                device_id=peer(-o), device_id_type=pl.DeviceIdType.MESH,
-            ).start()
+            send_part(m, o, -o, part_recv.at[m])
 
     def finish(m):
-        arrived(back.at[m], part_recv.at[m])
+        if m < micro - 1:
+            arrived(back.at[m], part_recv.at[m])
+        else:
+            @pl.when(first)
+            def _():
+                arrived(back.at[m], part_recv.at[m])
+
+            @pl.when(jnp.logical_not(first))
+            def _():
+                arrived(back.at[m, 1], part_recv.at[m])
         for which in range(2):
-            total = own[m, which]
-            for o in range(1, WINDOW):
-                total = total + back[m, o - 1, which].astype(jnp.float32)
-            kv_out[m, which] = total.astype(jnp.bfloat16)
+            total = own[m, which] + back[m, 1, which].astype(jnp.float32)
+            beside = back[m, 0, which].astype(jnp.float32)
+            if m == micro - 1:
+                beside = jnp.where(first, beside, 0.0)
+            kv_out[m, which] = (total + beside).astype(jnp.bfloat16)
 
     if True:
         log_load.wait()
@@ -182,24 +214,30 @@
             dq_own[c] = dot(grads, keys, ((0,), (0,)))
 
     if True:
-        arrived(kv.at[0, others], kv_recv.at[0])
+        take_kv(0, 0)
+    keys = far(0, 0)
+    if True:
+        for c in range(chunks):
+            pf[near_rows, lanes(c)] = probs_of(0, c, keys, near_rows)
+    if True:
+        take_kv(0, 1)
     for m in range(1, micro):
         arrived(kv.at[m, 0], kv_sem.at[m])
         send_kv(m)
-
-    keys, values = far(0, 0), far(0, 1)
+    values = far(0, 1)
     for c in range(chunks):
         if True:
             upstream = split(go[0, :, cols(c)])
-            probs = probs_of(0, c, keys, near_rows)
+            probs = pf[near_rows, lanes(c)]
             grads = grads_of(probs, values, upstream, row_dot[c])
-            pr[near_rows, lanes(c)] = probs.astype(jnp.bfloat16)
             ds[near_rows, lanes(c)] = grads
             put_dq(0, c, (dq_own[c] + dot(grads, keys, ((0,), (0,)))) * factor)
 
-            @pl.when(has_below)
+            @pl.when(has_below if c < KEEP else jnp.logical_and(has_below, first))
             def _(c=c):
                 hop(c).start()
+
+            pr[near_rows, lanes(c)] = probs.astype(jnp.bfloat16)
 
     if True:
         all_queries, all_upstream = stack(q[0]), stack(go[0])
@@ -211,44 +249,74 @@
 
     for m in range(1, micro):
         if True:
-            arrived(kv.at[m, others], kv_recv.at[m])
+            for which in range(2):
+                take_kv(m, which)
         keys = jnp.concatenate([kv[m, o, 0] for o in range(WINDOW)], axis=0)
         if True:
             for c in range(chunks):
                 pf[:, lanes(c)] = probs_of(m, c, keys, pl.ds(0, WINDOW * rows))
 
         far_values, own_values = far(m, 1), kv[m, 0, 1]
-        dk_far = dv_far = dk_own = dv_own = None
+        all_queries = stack(q[m])
+        ready = (chunks - 1) * span
+        dots, ups = [], []
         for c in range(chunks):
+            if c == chunks - 1:
+                if True:
+                    early = pl.ds(0, ready)
+                    far_sum[0] = dot(ds[near_rows, early], all_queries[:ready], ((1,), (0,)))
+                    far_sum[1] = dot(pr[near_rows, early], jnp.concatenate(ups, axis=0), ((1,), (0,)))
             if m == 1:
                 @pl.when(has_above)
                 def _(c=c):
                     if True:
                         hop(c).wait_recv()
             if True:
-                chunk = queries(m, c)
                 upstream = split((
                     go[m, :, cols(c)].astype(jnp.float32) + passed[c].astype(jnp.float32)
                 ).astype(jnp.bfloat16))
-                dots = row_dots(m, c, upstream)
+                ups.append(upstream)
+                dots.append(row_dots(m, c, upstream))
                 probs = pf[near_rows, lanes(c)]
-                grads = grads_of(probs, far_values, upstream, dots)
-                dk = dot(grads, chunk, ((1,), (0,)))
-                dv = dot(probs.astype(jnp.bfloat16), upstream, ((1,), (0,)))
-                dk_far = dk if dk_far is None else dk_far + dk
-                dv_far = dv if dv_far is None else dv_far + dv
-                if c == chunks - 1:
-                    send_parts(m, dk_far * factor, dv_far)
-            if True:
+                grads = grads_of(probs, far_values, upstream, dots[c])
+                ds[near_rows, lanes(c)] = grads
+                probs = probs.astype(jnp.bfloat16)
+                if c < chunks - 1:
+                    pr[near_rows, lanes(c)] = probs
+                else:
+                    dv = far_sum[1] + dot(probs, upstream, ((1,), (0,)))
+                    dk = (far_sum[0] + dot(grads, all_queries[ready:], ((1,), (0,)))) * factor
+                    for which, total in enumerate((dk, dv)):
+                        part[m, 0, which] = total[:rows].astype(jnp.bfloat16)
+
+                    @pl.when(first)
+                    def _():
+                        send_part(m, 1, 1, relay_recv)
+                        for which, total in enumerate((dk, dv)):
+                            part[m, 1, which] = total[rows:].astype(jnp.bfloat16)
+                        send_part(m, 2, -2, part_recv.at[m])
+
+                    @pl.when(jnp.logical_not(first))
+                    def _():
+                        send_part(m, 1, -1, part_recv.at[m])
+                        arrived(back.at[m, 0], relay_recv)
+                        for which, total in enumerate((dk, dv)):
+                            both = total[rows:] + back[m, 0, which].astype(jnp.float32)
+                            part[m, 1, which] = both.astype(jnp.bfloat16)
+                        send_part(m, 2, -2, part_recv.at[m])
+            for later, after in AFTER.items():
+                if after == c:
+                    @pl.when(jnp.logical_and(has_below, jnp.logical_not(first)))
+                    def _(later=later):
+                        hop(later).start()
+        if True:
+            for c in range(chunks):
                 probs = pf[own_rows, lanes(c)]
-                own_grads = grads_of(probs, own_values, upstream, dots)
-                dk = dot(own_grads, chunk, ((1,), (0,)))
-                dv = dot(probs.astype(jnp.bfloat16), upstream, ((1,), (0,)))
-                dk_own = dk if dk_own is None else dk_own + dk
-                dv_own = dv if dv_own is None else dv_own + dv
-                put_dq(m, c, dot(jnp.concatenate([own_grads, grads], axis=0), keys, ((0,), (0,))) * factor)
-        own[m, 0] = dk_own * factor
-        own[m, 1] = dv_own
+                ds[own_rows, lanes(c)] = grads_of(probs, own_values, ups[c], dots[c])
+                pr[own_rows, lanes(c)] = probs.astype(jnp.bfloat16)
+                put_dq(m, c, dot(ds[:, lanes(c)], keys, ((0,), (0,))) * factor)
+            own[m, 0] = dot(ds[own_rows, :], all_queries, ((1,), (0,))) * factor
+            own[m, 1] = dot(pr[own_rows, :], jnp.concatenate(ups, axis=0), ((1,), (0,)))
 
     for m in range(micro):
         if True:
@@ -323,9 +391,10 @@
                 pltpu.VMEM((WINDOW * rows, heads * rows), low),
                 pltpu.VMEM((WINDOW * rows, heads * rows), low),
                 pltpu.VMEM((WINDOW * rows, heads * rows), full),
+                pltpu.VMEM((2, others * rows, head), full),
                 pltpu.SMEM(block_order.shape, jnp.int32),
                 dma, dma, dma, dma((micro,)),
-                dma, dma((micro,)), dma, dma((micro,)), dma, dma((chunks,)),
+                dma, dma((micro,)), dma((micro,)), dma, dma((micro,)), dma, dma, dma((chunks,)),
             ],
             compiler_params=pltpu.CompilerParams(collective_id=0, has_side_effects=True),
         )(block_order, query_in, key_in, value_in, forward_out, grad_out, log_sum)

time: 19.9 us -> 19.1 us (0.960)
  the two profiles are of different devices: /device:TPU:1 before, /device:TPU:25 now
where the time goes in v2:
time: 19.1 us; the launch traced here: 18.9 us
  Pallas kernels  18.3 us (96%)
  between operations  0.64 us (3%)
    pallas_call x1, Pallas kernels, shards(): pl.pallas_call(functools.partial(kernel, members, sections, block_order.s...  17.4 us
    pallas_call x1, Pallas kernels, shards(): pl.pallas_call(writer, out_shape=(jax.ShapeDtypeStruct(query_in.shape, lo...  0.84 us

profile of v2, /device:TPU:25, one launch (start us, length us, event | category | flops | bytes accessed | tf_op | source)
XLA Modules:
  0.0 18.9 jit_solution(8410561328978054326)
XLA Ops:
  0.6 17.4 %shard_map.94 = (bf16[2,4,128,256]{3,2,1,0:T(8,128)(2,1)S(1)}, bf16[2,2,128,128]{3,2,1,0:T(8,128)(2,1)S(1)}) custom-call(s32[8]{0:T(128)} %order_hbm.1, bf16[1,2,128,1024]{3,2,1,0:T(8,128)(2,1)} %q_hbm.1, bf16[1,2,128,128]{3,2,1,0:T(8,128)(2,1)} %k_hbm.1, bf16[1,2,128,128]{3,2,1,0:T(8,128)(2,1)} %v_hbm.1, bf16[1,2,128,1024]{3,2,1,0:T(8,128)(2,1)} %fo_hbm.1, ...), custom_call_target="tpu_custom_call" | custom-call | tf_op jit(solution)/shard_map/pallas_call | solution.py:373
  18.1 0.8 %shard_map.95 = (bf16[1,2,128,1024]{3,2,1,0:T(8,128)(2,1)}, bf16[1,2,128,128]{3,2,1,0:T(8,128)(2,1)}, bf16[1,2,128,128]{3,2,1,0:T(8,128)(2,1)}) custom-call(bf16[2,4,128,256]{3,2,1,0:T(8,128)(2,1)S(1)} %get-tuple-element.5.dq, bf16[2,2,128,128]{3,2,1,0:T(8,128)(2,1)S(1)} %get-tuple-element.6.kv_out), custom_call_target="tpu_custom_call" | custom-call | tf_op jit(solution)/shard_map/pallas_call | solution.py:401

commit v3 on v2

--- a/solution.py
+++ b/solution.py
@@ -10,7 +10,8 @@
 
 WINDOW = 3
 KEEP = 2
-AFTER = {2: 1, 3: 1}
+YIELD = -1
+HOLD = 1
 LOG2E = math.log2(math.e)
 HIDE = -1e30
 
@@ -78,14 +79,11 @@
             device_id=peer(offset), device_id_type=pl.DeviceIdType.MESH,
         ).start()
 
-    def send_kv(m):
-        for which in range(2):
-            move_kv(m, 0, which, 2, 2)
-
-        @pl.when(first)
+    def send_kv(m, who):
+        @pl.when(who)
         def _():
             for which in range(2):
-                move_kv(m, 0, which, 1, 1)
+                move_kv(m, 0, which, 2, 2)
 
     def take_kv(m, which):
         arrived(kv.at[m, others, which], far_recv[which].at[m])
@@ -95,7 +93,14 @@
             move_kv(m, 2, which, -1, 1)
 
     arrived(kv.at[0, 0], kv_sem.at[0])
-    send_kv(0)
+
+    @pl.when(first)
+    def _():
+        for which in range(2):
+            move_kv(0, 0, which, 1, 1)
+    send_kv(0, jnp.logical_not(first))
+    if YIELD < 0:
+        send_kv(0, first)
 
     half = members * rows // blocks
     per = rows // half
@@ -167,9 +172,9 @@
             device_id=below, device_id_type=pl.DeviceIdType.MESH,
         )
 
-    def send_part(m, o, offset, recv_sem):
+    def send_piece(m, o, which, offset, recv_sem):
         pltpu.make_async_remote_copy(
-            src_ref=part.at[m, o - 1], dst_ref=back.at[m, o - 1],
+            src_ref=part.at[m, o - 1, which], dst_ref=back.at[m, o - 1, which],
             send_sem=part_send, recv_sem=recv_sem,
             device_id=peer(offset), device_id_type=pl.DeviceIdType.MESH,
         ).start()
@@ -178,7 +183,7 @@
         for o in range(WINDOW - 1, 0, -1):
             for which, total in enumerate((dk, dv)):
                 part[m, o - 1, which] = total[(o - 1) * rows:o * rows].astype(jnp.bfloat16)
-            send_part(m, o, -o, part_recv.at[m])
+                send_piece(m, o, which, -o, part_recv.at[m])
 
     def finish(m):
         if m < micro - 1:
@@ -212,6 +217,8 @@
             pr[own_rows, lanes(c)] = probs.astype(jnp.bfloat16)
             ds[own_rows, lanes(c)] = grads
             dq_own[c] = dot(grads, keys, ((0,), (0,)))
+            if c == YIELD:
+                send_kv(0, first)
 
     if True:
         take_kv(0, 0)
@@ -223,7 +230,13 @@
         take_kv(0, 1)
     for m in range(1, micro):
         arrived(kv.at[m, 0], kv_sem.at[m])
-        send_kv(m)
+        for which in range(2):
+            move_kv(m, 0, which, 2, 2)
+
+        @pl.when(first)
+        def _(m=m):
+            for which in range(2):
+                move_kv(m, 0, which, 1, 1)
     values = far(0, 1)
     for c in range(chunks):
         if True:
@@ -260,12 +273,33 @@
         all_queries = stack(q[m])
         ready = (chunks - 1) * span
         dots, ups = [], []
+
+        def send_held(who):
+            @pl.when(jnp.logical_and(has_below, jnp.logical_and(jnp.logical_not(first), who)))
+            def _():
+                for held in range(KEEP, chunks):
+                    hop(held).start()
+
+        def sum_far(start, stop):
+            early = pl.ds(start * span, (stop - start) * span)
+            for which, (left, right) in enumerate((
+                (ds, all_queries[start * span:stop * span]),
+                (pr, jnp.concatenate(ups[start:stop], axis=0)),
+            )):
+                total = dot(left[near_rows, early], right, ((1,), (0,)))
+                far_sum[which] = total if start == 0 else far_sum[which] + total
+
         for c in range(chunks):
+            if c == HOLD + 1:
+                if True:
+                    sum_far(0, c)
+                if m == 1:
+                    send_held(has_above)
             if c == chunks - 1:
                 if True:
-                    early = pl.ds(0, ready)
-                    far_sum[0] = dot(ds[near_rows, early], all_queries[:ready], ((1,), (0,)))
-                    far_sum[1] = dot(pr[near_rows, early], jnp.concatenate(ups, axis=0), ((1,), (0,)))
+                    sum_far(HOLD + 1, c)
+                if m == 1:
+                    send_held(jnp.logical_not(has_above))
             if m == 1:
                 @pl.when(has_above)
                 def _(c=c):
@@ -284,31 +318,26 @@
                 if c < chunks - 1:
                     pr[near_rows, lanes(c)] = probs
                 else:
-                    dv = far_sum[1] + dot(probs, upstream, ((1,), (0,)))
-                    dk = (far_sum[0] + dot(grads, all_queries[ready:], ((1,), (0,)))) * factor
-                    for which, total in enumerate((dk, dv)):
+                    sums = [None, None]
+                    sums[1] = far_sum[1] + dot(probs, upstream, ((1,), (0,)))
+                    sums[0] = (far_sum[0] + dot(grads, all_queries[ready:], ((1,), (0,)))) * factor
+                    for which in (1, 0):
+                        total = sums[which]
                         part[m, 0, which] = total[:rows].astype(jnp.bfloat16)
 
-                    @pl.when(first)
-                    def _():
-                        send_part(m, 1, 1, relay_recv)
-                        for which, total in enumerate((dk, dv)):
+                        @pl.when(first)
+                        def _(which=which, total=total):
+                            send_piece(m, 1, which, 1, relay_recv.at[which])
                             part[m, 1, which] = total[rows:].astype(jnp.bfloat16)
-                        send_part(m, 2, -2, part_recv.at[m])
-
-                    @pl.when(jnp.logical_not(first))
-                    def _():
-                        send_part(m, 1, -1, part_recv.at[m])
-                        arrived(back.at[m, 0], relay_recv)
-                        for which, total in enumerate((dk, dv)):
+                            send_piece(m, 2, which, -2, part_recv.at[m])
+
+                        @pl.when(jnp.logical_not(first))
+                        def _(which=which, total=total):
+                            send_piece(m, 1, which, -1, part_recv.at[m])
+                            arrived(back.at[m, 0, which], relay_recv.at[which])
                             both = total[rows:] + back[m, 0, which].astype(jnp.float32)
                             part[m, 1, which] = both.astype(jnp.bfloat16)
-                        send_part(m, 2, -2, part_recv.at[m])
-            for later, after in AFTER.items():
-                if after == c:
-                    @pl.when(jnp.logical_and(has_below, jnp.logical_not(first)))
-                    def _(later=later):
-                        hop(later).start()
+                            send_piece(m, 2, which, -2, part_recv.at[m])
         if True:
             for c in range(chunks):
                 probs = pf[own_rows, lanes(c)]
@@ -394,7 +423,7 @@
                 pltpu.VMEM((2, others * rows, head), full),
                 pltpu.SMEM(block_order.shape, jnp.int32),
                 dma, dma, dma, dma((micro,)),
-                dma, dma((micro,)), dma((micro,)), dma, dma((micro,)), dma, dma, dma((chunks,)),
+                dma, dma((micro,)), dma((micro,)), dma, dma((micro,)), dma((2,)), dma, dma((chunks,)),
             ],
             compiler_params=pltpu.CompilerParams(collective_id=0, has_side_effects=True),
         )(block_order, query_in, key_in, value_in, forward_out, grad_out, log_sum)

time: 19.1 us -> 18.6 us (0.974)
  the two profiles are of different devices: /device:TPU:25 before, /device:TPU:1 now
where the time goes in v3:
time: 18.6 us; the launch traced here: 18.4 us
  Pallas kernels  17.8 us (96%)
  between operations  0.64 us (3%)
    pallas_call x1, Pallas kernels, shards(): pl.pallas_call(functools.partial(kernel, members, sections, block_order.s...  16.9 us
    pallas_call x1, Pallas kernels, shards(): pl.pallas_call(writer, out_shape=(jax.ShapeDtypeStruct(query_in.shape, lo...  0.84 us

profile of v3, /device:TPU:1, one launch (start us, length us, event | category | flops | bytes accessed | tf_op | source)
XLA Modules:
  0.0 18.4 jit_solution(1244809996456457294)
XLA Ops:
  0.6 16.9 %shard_map.94 = (bf16[2,4,128,256]{3,2,1,0:T(8,128)(2,1)S(1)}, bf16[2,2,128,128]{3,2,1,0:T(8,128)(2,1)S(1)}) custom-call(s32[8]{0:T(128)} %order_hbm.1, bf16[1,2,128,1024]{3,2,1,0:T(8,128)(2,1)} %q_hbm.1, bf16[1,2,128,128]{3,2,1,0:T(8,128)(2,1)} %k_hbm.1, bf16[1,2,128,128]{3,2,1,0:T(8,128)(2,1)} %v_hbm.1, bf16[1,2,128,1024]{3,2,1,0:T(8,128)(2,1)} %fo_hbm.1, ...), custom_call_target="tpu_custom_call" | custom-call | tf_op jit(solution)/shard_map/pallas_call | solution.py:402
  17.6 0.8 %shard_map.95 = (bf16[1,2,128,1024]{3,2,1,0:T(8,128)(2,1)}, bf16[1,2,128,128]{3,2,1,0:T(8,128)(2,1)}, bf16[1,2,128,128]{3,2,1,0:T(8,128)(2,1)}) custom-call(bf16[2,4,128,256]{3,2,1,0:T(8,128)(2,1)S(1)} %get-tuple-element.5.dq, bf16[2,2,128,128]{3,2,1,0:T(8,128)(2,1)S(1)} %get-tuple-element.6.kv_out), custom_call_target="tpu_custom_call" | custom-call | tf_op jit(solution)/shard_map/pallas_call | solution.py:430

commit v4 on v3

v4 whole, which is shorter than its diff:
```python
import functools
import math

import jax
import jax.numpy as jnp
from jax import lax
from jax.experimental import pallas as pl
from jax.experimental.pallas import tpu as pltpu
from jax.sharding import PartitionSpec as P

WINDOW = 3
LOG2E = math.log2(math.e)
HIDE = -1e30


def dot(a, b, dims):
    return lax.dot_general(a, b, (dims, ((), ())), preferred_element_type=jnp.float32)


def plan_of(heads, group):
    return [(h, group) for h in range(0, heads, group)]


def kernel(
    members, sections, blocks,
    order_hbm, q_hbm, k_hbm, v_hbm, fo_hbm, go_hbm, log_hbm,
    dq, kv_out,
    rows_in, logs, kv, bias, passed, own, part, back, dq_own, ds, pr, pf, ups, far_sum, order,
    order_sem, rows_sem, log_sem, kv_sem,
    kv_send, k_recv, v_recv, part_send, part_recv, relay_recv, hop_send, hop_recv,
):
    _, micro, rows, width = rows_in.shape
    q, go, fo = rows_in.at[0], rows_in.at[1], rows_in.at[2]
    head = kv.shape[-1]
    heads = width // head
    group = bias.shape[1] // rows
    pairs = [(h, group) for h in range(0, heads, group)]
    plan = plan_of(heads, group)
    early = [h for h, _ in plan].index(heads // 2)
    factor = 1.0 / math.sqrt(head)
    me = lax.axis_index("ctx")
    sec = lax.axis_index("section")
    peer = lambda offset: {"ctx": lax.rem(me + offset + members, members)}
    below = {"section": jnp.maximum(sec - 1, 0)}
    above = {"section": jnp.minimum(sec + 1, sections - 1)}
    has_below = sec > 0
    has_above = sec < sections - 1
    first = lax.rem(me, 2) == 0
    yields = lax.rem(me, 4) == 0

    barrier = pltpu.get_barrier_semaphore()
    near = sorted({o % members for o in range(1 - WINDOW, WINDOW)} - {0})
    for o in near:
        pl.semaphore_signal(barrier, inc=1, device_id=peer(o), device_id_type=pl.DeviceIdType.MESH)

    @pl.when(has_above)
    def _():
        pl.semaphore_signal(barrier, inc=1, device_id=above, device_id_type=pl.DeviceIdType.MESH)

    def arrived(ref, sem):
        pltpu.make_async_copy(ref, ref, sem).wait()

    for m in range(micro):
        for which, source in enumerate((k_hbm, v_hbm)):
            pltpu.make_async_copy(source.at[0, m], kv.at[m, 0, which], kv_sem.at[m]).start()
    order_load = pltpu.make_async_copy(order_hbm, order, order_sem)
    order_load.start()
    log_load = pltpu.make_async_copy(log_hbm.at[0], logs, log_sem)
    log_load.start()
    for which, source in enumerate((q_hbm, go_hbm, fo_hbm)):
        pltpu.make_async_copy(source.at[0], rows_in.at[which], rows_sem).start()

    if True:
        pl.semaphore_wait(barrier, len(near) + has_below.astype(jnp.int32))

    others = pl.ds(1, WINDOW - 1)
    far_recv = (k_recv, v_recv)

    def move_kv(m, source, which, offset, slot):
        pltpu.make_async_remote_copy(
            src_ref=kv.at[m, source, which], dst_ref=kv.at[m, slot, which],
            send_sem=kv_send, recv_sem=far_recv[which].at[m],
            device_id=peer(offset), device_id_type=pl.DeviceIdType.MESH,
        ).start()

    def send_kv(m, which, who):
        @pl.when(who)
        def _():
            move_kv(m, 0, which, 2, 2)

    def take_kv(m, which):
        arrived(kv.at[m, others, which], far_recv[which].at[m])

        @pl.when(jnp.logical_not(first))
        def _():
            move_kv(m, 2, which, -1, 1)

    arrived(kv.at[0, 0], kv_sem.at[0])

    @pl.when(first)
    def _():
        for which in range(2):
            move_kv(0, 0, which, 1, 1)
    move_kv(0, 0, 0, 2, 2)
    send_kv(0, 1, jnp.logical_not(yields))

    half = members * rows // blocks
    per = rows // half
    lane = lax.broadcasted_iota(jnp.int32, (half, rows), 1)
    down = lax.broadcasted_iota(jnp.int32, (half, rows), 0)
    q_place = lax.rem(lane, half)
    order_load.wait()
    for b in range(per):
        base = order[me * per + b] * half
        q_place = q_place + jnp.where(lane // half == b, base, 0)
    for o in range(WINDOW):
        source = lax.rem(me - o + members, members)
        for b in range(per):
            k_place = down + order[source * per + b] * half
            tile = jnp.where(k_place <= q_place, 0.0, HIDE)
            for g in range(group):
                bias[pl.ds(o * rows + b * half, half), pl.ds(g * rows, rows)] = tile

    @pl.when(jnp.logical_not(has_above))
    def _():
        passed[...] = jnp.zeros_like(passed)

    ones = jnp.ones((8, head), jnp.bfloat16)
    near_rows = pl.ds(rows, (WINDOW - 1) * rows)
    own_rows = pl.ds(0, rows)

    def split(block):
        return jnp.concatenate([block[:, i:i + head] for i in range(0, block.shape[1], head)], axis=0)

    def cols(h, n):
        return pl.ds(h * head, n * head)

    def lanes(h, n):
        return pl.ds(h * rows, n * rows)

    def row_dots(upstream, saved):
        product = upstream.astype(jnp.float32) * saved.astype(jnp.float32)
        high = product.astype(jnp.bfloat16)
        low = (product - high.astype(jnp.float32)).astype(jnp.bfloat16)
        total = (dot(ones, high, ((1,), (1,))) + dot(ones, low, ((1,), (1,))))[0:1]
        return [total[:, i:i + rows] for i in range(0, total.shape[1], rows)]

    def joined(row_dot, h, n):
        return jnp.concatenate(row_dot[h:h + n], axis=1)

    def probs_of(m, h, n, keys, where):
        log_row = jnp.concatenate([logs[m, pl.ds(g, 1), :] for g in range(h, h + n)], axis=1) * LOG2E
        scores = dot(keys, split(q[m, :, cols(h, n)]), ((1,), (1,)))
        return jnp.exp2(scores * (factor * LOG2E) - log_row + bias[where, pl.ds(0, n * rows)])

    def far(m, which):
        return jnp.concatenate([kv[m, o, which] for o in range(1, WINDOW)], axis=0)

    def grads_of(probs, values, upstream, row_dot):
        return (probs * (dot(values, upstream, ((1,), (1,))) - row_dot)).astype(jnp.bfloat16)

    def put_dq(m, h, n, grad_query):
        for g in range(n):
            dq[m, h + g] = grad_query[g * rows:(g + 1) * rows].astype(jnp.bfloat16)

    def hop(c):
        part_of = pl.ds(*plan[c])
        return pltpu.make_async_remote_copy(
            src_ref=dq.at[0, part_of], dst_ref=passed.at[part_of],
            send_sem=hop_send, recv_sem=hop_recv.at[c],
            device_id=below, device_id_type=pl.DeviceIdType.MESH,
        )

    def send_piece(m, o, which, offset, recv_sem):
        pltpu.make_async_remote_copy(
            src_ref=part.at[m, o - 1, which], dst_ref=back.at[m, o - 1, which],
            send_sem=part_send, recv_sem=recv_sem,
            device_id=peer(offset), device_id_type=pl.DeviceIdType.MESH,
        ).start()

    def send_parts(m, dk, dv):
        for o in range(WINDOW - 1, 0, -1):
            for which, total in enumerate((dk, dv)):
                part[m, o - 1, which] = total[(o - 1) * rows:o * rows].astype(jnp.bfloat16)
                send_piece(m, o, which, -o, part_recv.at[m])

    def finish(m):
        if m < micro - 1:
            arrived(back.at[m], part_recv.at[m])
        else:
            @pl.when(first)
            def _():
                arrived(back.at[m], part_recv.at[m])

            @pl.when(jnp.logical_not(first))
            def _():
                arrived(back.at[m, 1], part_recv.at[m])
        for which in range(2):
            total = own[m, which] + back[m, 1, which].astype(jnp.float32)
            beside = back[m, 0, which].astype(jnp.float32)
            if m == micro - 1:
                beside = jnp.where(first, beside, 0.0)
            kv_out[m, which] = (total + beside).astype(jnp.bfloat16)

    if True:
        log_load.wait()
        arrived(rows_in, rows_sem)
    keys, values = kv[0, 0, 0], kv[0, 0, 1]
    row_dot = []
    if True:
        for h, n in pairs:
            upstream = split(go[0, :, cols(h, n)])
            row_dot += row_dots(upstream, split(fo[0, :, cols(h, n)]))
            probs = probs_of(0, h, n, keys, own_rows)
            grads = grads_of(probs, values, upstream, joined(row_dot, h, n))
            pr[own_rows, lanes(h, n)] = probs.astype(jnp.bfloat16)
            ds[own_rows, lanes(h, n)] = grads
            dq_own[lanes(h, n), :] = dot(grads, keys, ((0,), (0,)))
            if h == 0:
                send_kv(0, 1, yields)

    if True:
        take_kv(0, 0)
    keys = far(0, 0)
    if True:
        for h, n in plan[:1]:
            pf[near_rows, lanes(h, n)] = probs_of(0, h, n, keys, near_rows)
    if True:
        take_kv(0, 1)
    for m in range(1, micro):
        arrived(kv.at[m, 0], kv_sem.at[m])
        for which in range(2):
            move_kv(m, 0, which, 2, 2)

        @pl.when(first)
        def _(m=m):
            for which in range(2):
                move_kv(m, 0, which, 1, 1)
    values = far(0, 1)
    for c, (h, n) in enumerate(plan):
        if True:
            upstream = split(go[0, :, cols(h, n)])
            probs = pf[near_rows, lanes(h, n)] if c < 1 else probs_of(0, h, n, keys, near_rows)
            grads = grads_of(probs, values, upstream, joined(row_dot, h, n))
            ds[near_rows, lanes(h, n)] = grads
            put_dq(0, h, n, (dq_own[lanes(h, n), :] + dot(grads, keys, ((0,), (0,)))) * factor)

            @pl.when(has_below if c < early else jnp.logical_and(has_below, first))
            def _(c=c):
                hop(c).start()

            pr[near_rows, lanes(h, n)] = probs.astype(jnp.bfloat16)

    if True:
        all_queries, all_upstream = split(q[0]), split(go[0])
        dk = dot(ds[...], all_queries, ((1,), (0,))) * factor
        dv = dot(pr[...], all_upstream, ((1,), (0,)))
        send_parts(0, dk[rows:], dv[rows:])
        own[0, 0] = dk[:rows]
        own[0, 1] = dv[:rows]

    for m in range(1, micro):
        if True:
            for which in range(2):
                take_kv(m, which)
        keys = jnp.concatenate([kv[m, o, 0] for o in range(WINDOW)], axis=0)
        if True:
            for h, n in pairs:
                pf[:, lanes(h, n)] = probs_of(m, h, n, keys, pl.ds(0, WINDOW * rows))

        far_values, own_values = far(m, 1), kv[m, 0, 1]
        all_queries = split(q[m])
        row_dot = []

        def send_held(who):
            @pl.when(jnp.logical_and(has_below, jnp.logical_and(jnp.logical_not(first), who)))
            def _():
                for held in range(early, len(plan)):
                    hop(held).start()

        def key_sum(h, n):
            return dot(ds[near_rows, lanes(h, n)], all_queries[h * rows:(h + n) * rows], ((1,), (0,)))

        def value_sum(h, n):
            return dot(pr[near_rows, lanes(h, n)], ups[lanes(h, n), :], ((1,), (0,)))

        def send_sum(which, total):
            part[m, 0, which] = total[:rows].astype(jnp.bfloat16)

            @pl.when(first)
            def _():
                send_piece(m, 1, which, 1, relay_recv.at[which])
                part[m, 1, which] = total[rows:].astype(jnp.bfloat16)
                send_piece(m, 2, which, -2, part_recv.at[m])

            @pl.when(jnp.logical_not(first))
            def _():
                send_piece(m, 1, which, -1, part_recv.at[m])
                arrived(back.at[m, 0, which], relay_recv.at[which])
                both = total[rows:] + back[m, 0, which].astype(jnp.float32)
                part[m, 1, which] = both.astype(jnp.bfloat16)
                send_piece(m, 2, which, -2, part_recv.at[m])

        def sum_far(h, n):
            for which, total in enumerate((key_sum(h, n), value_sum(h, n))):
                far_sum[which] = total if h == 0 else far_sum[which] + total

        for c, (h, n) in enumerate(plan):
            if c == early:
                if True:
                    sum_far(0, h)
                if m == 1:
                    send_held(has_above)
            if c == len(plan) - 1:
                if True:
                    sum_far(plan[early][0], h - plan[early][0])
                if m == 1:
                    send_held(jnp.logical_not(has_above))
            if m == 1:
                @pl.when(has_above)
                def _(c=c):
                    if True:
                        hop(c).wait_recv()
            if True:
                upstream = (
                    split(go[m, :, cols(h, n)]).astype(jnp.float32)
                    + passed[h:h + n].reshape(n * rows, head).astype(jnp.float32)
                ).astype(jnp.bfloat16)
                ups[lanes(h, n), :] = upstream
                row_dot += row_dots(upstream, split(fo[m, :, cols(h, n)]))
                probs = pf[near_rows, lanes(h, n)]
                pr[near_rows, lanes(h, n)] = probs.astype(jnp.bfloat16)
                grad_probs = dot(far_values, upstream, ((1,), (1,))) - joined(row_dot, h, n)
                if c == len(plan) - 1:
                    send_sum(1, far_sum[1] + value_sum(h, n))
                ds[near_rows, lanes(h, n)] = (probs * grad_probs).astype(jnp.bfloat16)
                if c == len(plan) - 1:
                    send_sum(0, (far_sum[0] + key_sum(h, n)) * factor)
        if True:
            for h, n in pairs:
                at = lanes(h, n)
                probs = pf[own_rows, at]
                ds[own_rows, at] = grads_of(probs, own_values, ups[at, :], joined(row_dot, h, n))
                pr[own_rows, at] = probs.astype(jnp.bfloat16)
                put_dq(m, h, n, dot(ds[:, at], keys, ((0,), (0,))) * factor)
            own[m, 0] = dot(ds[own_rows, :], all_queries, ((1,), (0,))) * factor
            own[m, 1] = dot(pr[own_rows, :], ups[...], ((1,), (0,)))

    for m in range(micro):
        if True:
            finish(m)
    arrived(kv.at[:, others], kv_send)
    arrived(part, part_send)

    @pl.when(has_below)
    def _():
        arrived(passed, hop_send)


def writer(dq, kv_out, dq_hbm, dk_hbm, dv_hbm, sem):
    micro, heads, _, head = dq.shape
    for m in range(micro):
        for h in range(heads):
            pltpu.make_async_copy(
                dq.at[m, h], dq_hbm.at[0, m, :, pl.ds(h * head, head)], sem.at[0]
            ).start()
        for which, target in enumerate((dk_hbm, dv_hbm)):
            pltpu.make_async_copy(kv_out.at[m, which], target.at[0, m], sem.at[1]).start()
    pltpu.make_async_copy(dq, dq, sem.at[0]).wait()
    pltpu.make_async_copy(kv_out, kv_out, sem.at[1]).wait()


def solution(mesh):
    members = mesh.shape["ctx"]
    sections = mesh.shape["section"]
    in_specs = (
        P("section", None, "ctx", None),
        P("section", None, "ctx", None),
        P("section", None, "ctx", None),
        P("section", None, "ctx", None),
        P("section", None, None, "ctx"),
        P("section", None, "ctx", None),
        P(),
    )
    out_specs = (
        P("section", None, "ctx", None),
        P("section", None, "ctx", None),
        P("section", None, "ctx", None),
    )

    def shards(query_in, key_in, value_in, forward_out, log_sum, grad_out, block_order):
        _, micro, rows, width = query_in.shape
        head = key_in.shape[3]
        heads = width // head
        group = 2 if heads % 2 == 0 else 1
        low, full = jnp.bfloat16, jnp.float32
        dma = pltpu.SemaphoreType.DMA
        others = WINDOW - 1
        dq, kv_out = pl.pallas_call(
            functools.partial(kernel, members, sections, block_order.shape[0]),
            out_shape=(
                pltpu.VMEM((micro, heads, rows, head), low),
                pltpu.VMEM((micro, 2, rows, head), low),
            ),
            in_specs=[pl.BlockSpec(memory_space=pl.ANY)] * 7,
            out_specs=[pl.BlockSpec(memory_space=pltpu.VMEM)] * 2,
            scratch_shapes=[
                pltpu.VMEM((3, micro, rows, width), low),
                pltpu.VMEM((micro, heads, rows), full),
                pltpu.VMEM((micro, WINDOW, 2, rows, head), low),
                pltpu.VMEM((WINDOW * rows, group * rows), full),
                pltpu.VMEM((heads, rows, head), low),
                pltpu.VMEM((micro, 2, rows, head), full),
                pltpu.VMEM((micro, others, 2, rows, head), low),
                pltpu.VMEM((micro, others, 2, rows, head), low),
                pltpu.VMEM((heads * rows, head), full),
                pltpu.VMEM((WINDOW * rows, heads * rows), low),
                pltpu.VMEM((WINDOW * rows, heads * rows), low),
                pltpu.VMEM((WINDOW * rows, heads * rows), full),
                pltpu.VMEM((heads * rows, head), low),
                pltpu.VMEM((2, others * rows, head), full),
                pltpu.SMEM(block_order.shape, jnp.int32),
                dma, dma, dma, dma((micro,)),
                dma, dma((micro,)), dma((micro,)), dma, dma((micro,)), dma((2,)), dma, dma((len(plan_of(heads, group)),)),
            ],
            compiler_params=pltpu.CompilerParams(collective_id=0, has_side_effects=True),
        )(block_order, query_in, key_in, value_in, forward_out, grad_out, log_sum)
        return pl.pallas_call(
            writer,
            out_shape=(
                jax.ShapeDtypeStruct(query_in.shape, low),
                jax.ShapeDtypeStruct(key_in.shape, low),
                jax.ShapeDtypeStruct(value_in.shape, low),
            ),
            in_specs=[pl.BlockSpec(memory_space=pltpu.VMEM)] * 2,
            out_specs=[pl.BlockSpec(memory_space=pl.ANY)] * 3,
            scratch_shapes=[dma((2,))],
        )(*(pltpu.with_memory_space_constraint(x, pltpu.VMEM) for x in (dq, kv_out)))

    return jax.shard_map(shards, mesh=mesh, in_specs=in_specs, out_specs=out_specs, check_vma=False)
```

time: 18.6 us -> 18.4 us (0.989)
  Pallas kernels: 17.8 us -> 17.6 us
where the time goes in v4:
time: 18.4 us; the launch traced here: 18.3 us
  Pallas kernels  17.6 us (96%)
  between operations  0.64 us (3%)
    pallas_call x1, Pallas kernels, shards(): pl.pallas_call(functools.partial(kernel, members, sections, block_order.s...  16.8 us
    pallas_call x1, Pallas kernels, shards(): pl.pallas_call(writer, out_shape=(jax.ShapeDtypeStruct(query_in.shape, lo...  0.84 us

profile of v4, /device:TPU:1, one launch (start us, length us, event | category | flops | bytes accessed | tf_op | source)
XLA Modules:
  0.0 18.3 jit_solution(5718138766065319647)
XLA Ops:
  0.6 16.8 %shard_map.94 = (bf16[2,8,128,128]{3,2,1,0:T(8,128)(2,1)S(1)}, bf16[2,2,128,128]{3,2,1,0:T(8,128)(2,1)S(1)}) custom-call(s32[8]{0:T(128)} %order_hbm.1, bf16[1,2,128,1024]{3,2,1,0:T(8,128)(2,1)} %q_hbm.1, bf16[1,2,128,128]{3,2,1,0:T(8,128)(2,1)} %k_hbm.1, bf16[1,2,128,128]{3,2,1,0:T(8,128)(2,1)} %v_hbm.1, bf16[1,2,128,1024]{3,2,1,0:T(8,128)(2,1)} %fo_hbm.1, ...), custom_call_target="tpu_custom_call" | custom-call | tf_op jit(solution)/shard_map/pallas_call | solution.py:399
  17.4 0.8 %shard_map.95 = (bf16[1,2,128,1024]{3,2,1,0:T(8,128)(2,1)}, bf16[1,2,128,128]{3,2,1,0:T(8,128)(2,1)}, bf16[1,2,128,128]{3,2,1,0:T(8,128)(2,1)}) custom-call(bf16[2,8,128,128]{3,2,1,0:T(8,128)(2,1)S(1)} %get-tuple-element.5.dq, bf16[2,2,128,128]{3,2,1,0:T(8,128)(2,1)S(1)} %get-tuple-element.6.kv_out), custom_call_target="tpu_custom_call" | custom-call | tf_op jit(solution)/shard_map/pallas_call | solution.py:428

commit v5 on v4

--- a/solution.py
+++ b/solution.py
@@ -9,6 +9,7 @@
 from jax.sharding import PartitionSpec as P
 
 WINDOW = 3
+DONE = 1
 LOG2E = math.log2(math.e)
 HIDE = -1e30
 
@@ -70,8 +71,7 @@
     for which, source in enumerate((q_hbm, go_hbm, fo_hbm)):
         pltpu.make_async_copy(source.at[0], rows_in.at[which], rows_sem).start()
 
-    if True:
-        pl.semaphore_wait(barrier, len(near) + has_below.astype(jnp.int32))
+    pl.semaphore_wait(barrier, len(near) + has_below.astype(jnp.int32))
 
     others = pl.ds(1, WINDOW - 1)
     far_recv = (k_recv, v_recv)
@@ -202,31 +202,26 @@
                 beside = jnp.where(first, beside, 0.0)
             kv_out[m, which] = (total + beside).astype(jnp.bfloat16)
 
-    if True:
-        log_load.wait()
-        arrived(rows_in, rows_sem)
+    log_load.wait()
+    arrived(rows_in, rows_sem)
     keys, values = kv[0, 0, 0], kv[0, 0, 1]
     row_dot = []
-    if True:
-        for h, n in pairs:
-            upstream = split(go[0, :, cols(h, n)])
-            row_dot += row_dots(upstream, split(fo[0, :, cols(h, n)]))
-            probs = probs_of(0, h, n, keys, own_rows)
-            grads = grads_of(probs, values, upstream, joined(row_dot, h, n))
-            pr[own_rows, lanes(h, n)] = probs.astype(jnp.bfloat16)
-            ds[own_rows, lanes(h, n)] = grads
-            dq_own[lanes(h, n), :] = dot(grads, keys, ((0,), (0,)))
-            if h == 0:
-                send_kv(0, 1, yields)
-
-    if True:
-        take_kv(0, 0)
+    for h, n in pairs:
+        upstream = split(go[0, :, cols(h, n)])
+        row_dot += row_dots(upstream, split(fo[0, :, cols(h, n)]))
+        probs = probs_of(0, h, n, keys, own_rows)
+        grads = grads_of(probs, values, upstream, joined(row_dot, h, n))
+        pr[own_rows, lanes(h, n)] = probs.astype(jnp.bfloat16)
+        ds[own_rows, lanes(h, n)] = grads
+        dq_own[lanes(h, n), :] = dot(grads, keys, ((0,), (0,)))
+        if h == 0:
+            send_kv(0, 1, yields)
+
+    take_kv(0, 0)
     keys = far(0, 0)
-    if True:
-        for h, n in plan[:1]:
-            pf[near_rows, lanes(h, n)] = probs_of(0, h, n, keys, near_rows)
-    if True:
-        take_kv(0, 1)
+    for h, n in plan[:1]:
+        pf[near_rows, lanes(h, n)] = probs_of(0, h, n, keys, near_rows)
+    take_kv(0, 1)
     for m in range(1, micro):
         arrived(kv.at[m, 0], kv_sem.at[m])
         for which in range(2):
@@ -238,35 +233,31 @@
                 move_kv(m, 0, which, 1, 1)
     values = far(0, 1)
     for c, (h, n) in enumerate(plan):
-        if True:
-            upstream = split(go[0, :, cols(h, n)])
-            probs = pf[near_rows, lanes(h, n)] if c < 1 else probs_of(0, h, n, keys, near_rows)
-            grads = grads_of(probs, values, upstream, joined(row_dot, h, n))
-            ds[near_rows, lanes(h, n)] = grads
-            put_dq(0, h, n, (dq_own[lanes(h, n), :] + dot(grads, keys, ((0,), (0,)))) * factor)
-
-            @pl.when(has_below if c < early else jnp.logical_and(has_below, first))
-            def _(c=c):
-                hop(c).start()
-
-            pr[near_rows, lanes(h, n)] = probs.astype(jnp.bfloat16)
-
-    if True:
-        all_queries, all_upstream = split(q[0]), split(go[0])
-        dk = dot(ds[...], all_queries, ((1,), (0,))) * factor
-        dv = dot(pr[...], all_upstream, ((1,), (0,)))
-        send_parts(0, dk[rows:], dv[rows:])
-        own[0, 0] = dk[:rows]
-        own[0, 1] = dv[:rows]
+        upstream = split(go[0, :, cols(h, n)])
+        probs = pf[near_rows, lanes(h, n)] if c < 1 else probs_of(0, h, n, keys, near_rows)
+        grads = grads_of(probs, values, upstream, joined(row_dot, h, n))
+        ds[near_rows, lanes(h, n)] = grads
+        put_dq(0, h, n, (dq_own[lanes(h, n), :] + dot(grads, keys, ((0,), (0,)))) * factor)
+
+        @pl.when(has_below if c < early else jnp.logical_and(has_below, first))
+        def _(c=c):
+            hop(c).start()
+
+        pr[near_rows, lanes(h, n)] = probs.astype(jnp.bfloat16)
+
+    all_queries, all_upstream = split(q[0]), split(go[0])
+    dk = dot(ds[...], all_queries, ((1,), (0,))) * factor
+    dv = dot(pr[...], all_upstream, ((1,), (0,)))
+    send_parts(0, dk[rows:], dv[rows:])
+    own[0, 0] = dk[:rows]
+    own[0, 1] = dv[:rows]
 
     for m in range(1, micro):
-        if True:
-            for which in range(2):
-                take_kv(m, which)
+        for which in range(2):
+            take_kv(m, which)
         keys = jnp.concatenate([kv[m, o, 0] for o in range(WINDOW)], axis=0)
-        if True:
-            for h, n in pairs:
-                pf[:, lanes(h, n)] = probs_of(m, h, n, keys, pl.ds(0, WINDOW * rows))
+        for h, n in pairs:
+            pf[:, lanes(h, n)] = probs_of(m, h, n, keys, pl.ds(0, WINDOW * rows))
 
         far_values, own_values = far(m, 1), kv[m, 0, 1]
         all_queries = split(q[m])
@@ -301,54 +292,55 @@
                 part[m, 1, which] = both.astype(jnp.bfloat16)
                 send_piece(m, 2, which, -2, part_recv.at[m])
 
+        def own_grads(h, n):
+            at = lanes(h, n)
+            probs = pf[own_rows, at]
+            ds[own_rows, at] = grads_of(probs, own_values, ups[at, :], joined(row_dot, h, n))
+            pr[own_rows, at] = probs.astype(jnp.bfloat16)
+
         def sum_far(h, n):
             for which, total in enumerate((key_sum(h, n), value_sum(h, n))):
                 far_sum[which] = total if h == 0 else far_sum[which] + total
 
         for c, (h, n) in enumerate(plan):
             if c == early:
-                if True:
-                    sum_far(0, h)
+                sum_far(0, h)
+                for done, count in pairs[:DONE]:
+                    own_grads(done, count)
                 if m == 1:
                     send_held(has_above)
             if c == len(plan) - 1:
-                if True:
-                    sum_far(plan[early][0], h - plan[early][0])
+                sum_far(plan[early][0], h - plan[early][0])
                 if m == 1:
                     send_held(jnp.logical_not(has_above))
             if m == 1:
                 @pl.when(has_above)
                 def _(c=c):
-                    if True:
-                        hop(c).wait_recv()
-            if True:
-                upstream = (
-                    split(go[m, :, cols(h, n)]).astype(jnp.float32)
-                    + passed[h:h + n].reshape(n * rows, head).astype(jnp.float32)
-                ).astype(jnp.bfloat16)
-                ups[lanes(h, n), :] = upstream
-                row_dot += row_dots(upstream, split(fo[m, :, cols(h, n)]))
-                probs = pf[near_rows, lanes(h, n)]
-                pr[near_rows, lanes(h, n)] = probs.astype(jnp.bfloat16)
-                grad_probs = dot(far_values, upstream, ((1,), (1,))) - joined(row_dot, h, n)
-                if c == len(plan) - 1:
-                    send_sum(1, far_sum[1] + value_sum(h, n))
-                ds[near_rows, lanes(h, n)] = (probs * grad_probs).astype(jnp.bfloat16)
-                if c == len(plan) - 1:
-                    send_sum(0, (far_sum[0] + key_sum(h, n)) * factor)
-        if True:
-            for h, n in pairs:
-                at = lanes(h, n)
-                probs = pf[own_rows, at]
-                ds[own_rows, at] = grads_of(probs, own_values, ups[at, :], joined(row_dot, h, n))
-                pr[own_rows, at] = probs.astype(jnp.bfloat16)
-                put_dq(m, h, n, dot(ds[:, at], keys, ((0,), (0,))) * factor)
-            own[m, 0] = dot(ds[own_rows, :], all_queries, ((1,), (0,))) * factor
-            own[m, 1] = dot(pr[own_rows, :], ups[...], ((1,), (0,)))
+                    hop(c).wait_recv()
+            upstream = (
+                split(go[m, :, cols(h, n)]).astype(jnp.float32)
+                + passed[h:h + n].reshape(n * rows, head).astype(jnp.float32)
+            ).astype(jnp.bfloat16)
+            ups[lanes(h, n), :] = upstream
+            row_dot += row_dots(upstream, split(fo[m, :, cols(h, n)]))
+            probs = pf[near_rows, lanes(h, n)]
+            pr[near_rows, lanes(h, n)] = probs.astype(jnp.bfloat16)
+            grad_probs = dot(far_values, upstream, ((1,), (1,))) - joined(row_dot, h, n)
+            if c == len(plan) - 1:
+                send_sum(1, far_sum[1] + value_sum(h, n))
+            ds[near_rows, lanes(h, n)] = (probs * grad_probs).astype(jnp.bfloat16)
+            if c == len(plan) - 1:
+                send_sum(0, (far_sum[0] + key_sum(h, n)) * factor)
+        for h, n in pairs:
+            at = lanes(h, n)
+            if h >= DONE * group:
+                own_grads(h, n)
+            put_dq(m, h, n, dot(ds[:, at], keys, ((0,), (0,))) * factor)
+        own[m, 0] = dot(ds[own_rows, :], all_queries, ((1,), (0,))) * factor
+        own[m, 1] = dot(pr[own_rows, :], ups[...], ((1,), (0,)))
 
     for m in range(micro):
-        if True:
-            finish(m)
+        finish(m)
     arrived(kv.at[:, others], kv_send)
     arrived(part, part_send)
 

time: 18.4 us -> 18.4 us (level)
  no operation moved by 1% of the time
where the time goes in v5:
time: 18.4 us; the launch traced here: 18.3 us
  Pallas kernels  17.6 us (96%)
  between operations  0.64 us (3%)
    pallas_call x1, Pallas kernels, shards(): pl.pallas_call(functools.partial(kernel, members, sections, block_order.s...  16.8 us
    pallas_call x1, Pallas kernels, shards(): pl.pallas_call(writer, out_shape=(jax.ShapeDtypeStruct(query_in.shape, lo...  0.84 us

profile of v5, /device:TPU:1, one launch (start us, length us, event | category | flops | bytes accessed | tf_op | source)
XLA Modules:
  0.0 18.3 jit_solution(3990028270889052169)
XLA Ops:
  0.6 16.8 %shard_map.94 = (bf16[2,8,128,128]{3,2,1,0:T(8,128)(2,1)S(1)}, bf16[2,2,128,128]{3,2,1,0:T(8,128)(2,1)S(1)}) custom-call(s32[8]{0:T(128)} %order_hbm.1, bf16[1,2,128,1024]{3,2,1,0:T(8,128)(2,1)} %q_hbm.1, bf16[1,2,128,128]{3,2,1,0:T(8,128)(2,1)} %k_hbm.1, bf16[1,2,128,128]{3,2,1,0:T(8,128)(2,1)} %v_hbm.1, bf16[1,2,128,1024]{3,2,1,0:T(8,128)(2,1)} %fo_hbm.1, ...), custom_call_target="tpu_custom_call" | custom-call | tf_op jit(solution)/shard_map/pallas_call | solution.py:391
  17.4 0.8 %shard_map.95 = (bf16[1,2,128,1024]{3,2,1,0:T(8,128)(2,1)}, bf16[1,2,128,128]{3,2,1,0:T(8,128)(2,1)}, bf16[1,2,128,128]{3,2,1,0:T(8,128)(2,1)}) custom-call(bf16[2,8,128,128]{3,2,1,0:T(8,128)(2,1)S(1)} %get-tuple-element.5.dq, bf16[2,2,128,128]{3,2,1,0:T(8,128)(2,1)S(1)} %get-tuple-element.6.kv_out), custom_call_target="tpu_custom_call" | custom-call | tf_op jit(solution)/shard_map/pallas_call | solution.py:420
